TPU v7x, 32 devices: a whole 2x2x4 slice. The times are simulated.
32 devices in a mesh: seq: 8 (over z, y), tp: 4 (over x, core).
Axes of the slice: x: 2, y: 2, z: 4, core: 2. Of those that a mesh axis runs over, the one named last changes fastest.
Arguments:
- tokens: bfloat16 [8192, 1024], P(('seq', 'tp')), may hold values from -6 to 6
- fine_gain: float32 [1024], replicated, may hold values from 0.1 to 1.9
- fine_query: bfloat16 [1024, 1024], replicated, may hold values from -2.0625 to 2.0625
- fine_keyval: bfloat16 [1024, 2048], replicated, may hold values from -0.125 to 0.125
- fine_out: bfloat16 [1024, 1024], replicated, may hold values from -0.1875 to 0.1875
- down_weight: bfloat16 [1024, 4096], P(None, 'tp'), may hold values from -0.1875 to 0.1875
- coarse_gain: float32 [4096], replicated, may hold values from 0.1 to 1.9
- coarse_query: bfloat16 [4096, 4096], P('seq', 'tp'), may hold values from -1.03125 to 1.03125
- coarse_keyval: bfloat16 [4096, 2, 4096], P('seq', None, 'tp'), may hold values from -0.0625 to 0.0625
- coarse_out: bfloat16 [4096, 4096], P('tp'), may hold values from -0.09375 to 0.09375
- up_weight: bfloat16 [4096, 1024], P('tp'), may hold values from -0.09375 to 0.09375
Outputs:
- result: bfloat16 [8192, 1024], P(('seq', 'tp'))
All inputs are finite; a program needn't handle non-finite values.
Results may differ from a plain program's by a relative error of at most 0.02.
Values may be sent and summed in bfloat16 or wider, within the bound.
A program may use at most 192 MiB of HBM per device.

v0:
```python
import math

import jax
import jax.numpy as jnp
from jax import lax
from jax.sharding import PartitionSpec as P

HEAD = 128
WINDOW = 256
SHORT = 8


epsilon = 1e-06
big_negative = -1e30


def from_behind(array, axis, by):
    size = lax.axis_size(axis)
    pairs = [(i, i + by) for i in range(size) if 0 <= i + by < size]
    return lax.ppermute(array, axis, pairs)


def normalize(values, scale_gain):
    mean_square = jnp.mean(values * values, axis=-1, keepdims=True)
    return values * lax.rsqrt(mean_square + epsilon) * scale_gain


def online_update(state, query_heads, key_piece, value_piece, query_index):
    running_max, running_sum, accumulate = state
    scale = 1.0 / math.sqrt(HEAD)
    scores = (
        jnp.einsum("qhd,khd->hqk", query_heads, key_piece, preferred_element_type=jnp.float32)
        * scale
    )
    key_index = jnp.arange(key_piece.shape[0], dtype=jnp.int32)
    allowed = key_index[None, :] <= query_index[:, None]
    scores = jnp.where(allowed[None], scores, big_negative)
    new_max = jnp.maximum(running_max, jnp.max(scores, axis=-1))
    terms = jnp.where(allowed[None], jnp.exp(scores - new_max[..., None]), 0.0)
    new_sum = jnp.sum(terms, axis=-1)
    product = jnp.einsum(
        "hqk,khd->hqd", terms.astype(jnp.bfloat16), value_piece, preferred_element_type=jnp.float32
    )
    return (new_max, new_sum, product)


def body(
    tokens,
    fine_gain,
    fine_query,
    fine_keyval,
    fine_out,
    down_weight,
    coarse_gain,
    coarse_query,
    coarse_keyval,
    coarse_out,
    up_weight,
):
    tok_rows = tokens.shape[0]
    width = tokens.shape[1]
    fine_heads = width // HEAD
    scale = 1.0 / math.sqrt(HEAD)
    start_row = lax.axis_index(("seq", "tp")) * tok_rows
    inputs = tokens.astype(jnp.float32)
    normed = normalize(inputs, fine_gain).astype(jnp.bfloat16)
    queries = jnp.dot(normed, fine_query, preferred_element_type=jnp.float32).astype(jnp.bfloat16)
    keyvals = jnp.dot(normed, fine_keyval, preferred_element_type=jnp.float32).astype(jnp.bfloat16)
    earlier = from_behind(keyvals, ("seq", "tp"), 1)
    key_rows = jnp.concatenate([earlier, keyvals], 0)
    span = key_rows.shape[0]
    key_heads = key_rows[:, :width].reshape(span, fine_heads, HEAD)
    value_heads = key_rows[:, width:].reshape(span, fine_heads, HEAD)
    query_heads = queries.reshape(tok_rows, fine_heads, HEAD)
    scores = (
        jnp.einsum("qhd,khd->hqk", query_heads, key_heads, preferred_element_type=jnp.float32)
        * scale
    )
    row_index = jnp.arange(tok_rows, dtype=jnp.int32)[:, None]
    col_index = jnp.arange(span, dtype=jnp.int32)[None, :]
    offset = row_index + WINDOW - col_index
    allowed = (offset >= 0) & (offset < WINDOW) & (start_row - WINDOW + col_index >= 0)
    scores = jnp.where(allowed[None], scores, big_negative)
    peak = jnp.max(scores, axis=-1, keepdims=True)
    terms = jnp.where(allowed[None], jnp.exp(scores - peak), 0.0)
    denom = jnp.sum(terms, axis=-1)
    mixed = jnp.einsum(
        "hqk,khd->qhd", terms.astype(jnp.bfloat16), value_heads, preferred_element_type=jnp.float32
    )
    local = (mixed / jnp.transpose(denom)[..., None]).reshape(tok_rows, width).astype(jnp.bfloat16)
    fine_state = (inputs + jnp.dot(local, fine_out, preferred_element_type=jnp.float32)).astype(
        jnp.bfloat16
    )
    pooled = jnp.mean(
        fine_state.astype(jnp.float32).reshape(tok_rows // SHORT, SHORT, width), axis=1
    ).astype(jnp.bfloat16)
    pooled_all = lax.all_gather(pooled, "tp", axis=0, tiled=True)
    short_cols = jnp.dot(pooled_all, down_weight, preferred_element_type=jnp.float32).astype(
        jnp.bfloat16
    )
    shortened = lax.all_gather(short_cols, "tp", axis=1, tiled=True)
    coarse_normed = normalize(shortened.astype(jnp.float32), coarse_gain).astype(jnp.bfloat16)
    coarse_rows = coarse_normed.shape[0]
    local_cols = coarse_query.shape[1]
    local_heads = local_cols // HEAD
    query_rows = lax.all_gather(coarse_query, "seq", axis=0, tiled=True)
    keyval_rows = lax.all_gather(coarse_keyval, "seq", axis=0, tiled=True)
    count = query_rows.shape[0]
    query_sum = jnp.dot(coarse_normed, query_rows, preferred_element_type=jnp.float32)
    keyval_sum = jnp.dot(
        coarse_normed,
        keyval_rows.reshape(count, 2 * local_cols),
        preferred_element_type=jnp.float32,
    )
    coarse_queries = query_sum.astype(jnp.bfloat16).reshape(coarse_rows, local_heads, HEAD)
    coarse_kv = keyval_sum.astype(jnp.bfloat16).reshape(coarse_rows, 2, local_cols)
    my_first = lax.axis_index("seq") * coarse_rows
    query_index = my_first + jnp.arange(coarse_rows, dtype=jnp.int32)
    initial = (
        jnp.full((local_heads, coarse_rows), big_negative, jnp.float32),
        jnp.zeros((local_heads, coarse_rows), jnp.float32),
        jnp.zeros((local_heads, coarse_rows, HEAD), jnp.float32),
    )
    piece = lax.all_gather(coarse_kv, "seq", axis=0, tiled=True)
    count = piece.shape[0]
    key_piece = piece[:, 0].reshape(count, local_heads, HEAD)
    value_piece = piece[:, 1].reshape(count, local_heads, HEAD)
    final = lax.cond(
        jnp.int32(0) < my_first + coarse_rows,
        lambda: online_update(initial, coarse_queries, key_piece, value_piece, query_index),
        lambda: initial,
    )
    head_out = final[2] / final[1][..., None]
    coarse_heads = (
        jnp.transpose(head_out, (1, 0, 2)).reshape(coarse_rows, local_cols).astype(jnp.bfloat16)
    )
    partials = jnp.dot(coarse_heads, coarse_out, preferred_element_type=jnp.float32)
    attended = lax.psum_scatter(
        partials.astype(jnp.bfloat16), "tp", scatter_dimension=1, tiled=True
    ).astype(jnp.float32)
    coarse_state = (short_cols.astype(jnp.float32) + attended).astype(jnp.bfloat16)
    prior_row = from_behind(coarse_state[coarse_rows - 1 :], "seq", 1)
    delayed = jnp.concatenate([prior_row, coarse_state[: coarse_rows - 1]], 0)
    lifted = lax.psum_scatter(
        jnp.dot(delayed, up_weight, preferred_element_type=jnp.float32).astype(jnp.bfloat16),
        "tp",
        scatter_dimension=0,
        tiled=True,
    ).astype(jnp.float32)
    result = fine_state.astype(jnp.float32) + jnp.repeat(lifted, SHORT, axis=0)
    return result.astype(jnp.bfloat16)


def solution(mesh):
    return jax.shard_map(
        body,
        mesh=mesh,
        in_specs=(
            P(("seq", "tp"), None),
            P(),
            P(),
            P(),
            P(),
            P(None, "tp"),
            P(),
            P("seq", "tp"),
            P("seq", None, "tp"),
            P("tp", None),
            P("tp", None),
        ),
        out_specs=P(("seq", "tp"), None),
        check_vma=False,
    )
```

profile of v0, /device:TPU:0, one launch (start us, length us, event | category | flops | bytes accessed | tf_op | source)
XLA Modules:
  0.0 569.1 jit_solution(18229538027366523485)
XLA Ops:
  6.5 1.4 fusion.39
  7.9 4.7 convolution_convert_fusion.1
  12.7 3.4 collective-permute-start
  16.0 0.2 fusion.52
  16.3 3.1 fusion.36
  19.4 2.7 fusion.46
  22.1 1.3 copy.34
  23.5 2.1 fusion.43
  25.6 2.5 fusion.64
  28.1 0.8 fusion.33
  28.9 0.2 copy-done.6
  29.1 0.9 fusion.37
  30.1 16.9 %all_gather.15 = bf16[128,1024]{1,0:T(8,128)(2,1)S(1)} all-gather(bf16[32,1024]{1,0:T(8,128)(2,1)S(1)} %multiply_convert_fusion), channel_id=1, replica_groups=mesh['seq'=8,'tp'=4] {'tp'}, dimensions={0}, use_global_device_ids=true | all-gather | bytes 327680 | tf_op jit(solution)/shard_map/all_gather | solution.py:97
  46.9 1.2 convolution_convert_fusion.6
  48.1 0.0 all-gather.5.cloned.1.call-update
  48.1 0.0 all-gather.9.cloned.1.call-start
  48.2 0.7 all-gather.9.cloned.1.call-update
  48.9 0.0 all-gather.7.cloned.1.call-start
  48.9 0.7 all-gather.7.cloned.1.call-update
  49.6 0.0 all-gather.11.cloned.1.call-start
  49.7 16.6 %all-gather.5.cloned.1.call-done = bf16[128,4096]{1,0:T(8,128)(2,1)} async-done(((bf16[128,1024]{1,0:T(8,128)(2,1)}), bf16[128,4096]{1,0:T(8,128)(2,1)}) %all-gather.5.cloned.1.call-update) | async-done | bytes 1048592 | tf_op jit(solution)/shard_map/all_gather | solution.py:101
  66.3 1.5 fusion.18
  67.8 227.9 %all-gather.9.cloned.1.call-done = bf16[4096,2,1024]{2,1,0:T(2,128)(2,1)} async-done(((bf16[512,2,1024]{2,1,0:T(2,128)(2,1)}), bf16[4096,2,1024]{2,1,0:T(2,128)(2,1)}) %all-gather.9.cloned.1.call-update) | async-done | bytes 16777232 | tf_op jit(solution)/shard_map/all_gather | solution.py:107
  295.7 12.3 %copy.41 = bf16[512,8,2,1024]{3,1,2,0:T(8,128)(2,1)S(1)} copy(bf16[512,8,2,1024]{3,2,1,0:T(2,128)(2,1)} %bitcast.59) | data formatting | bytes 33554432
  308.1 2.6 convolution_convert_fusion.2
  310.6 1.0 copy.35
  311.6 0.0 all-gather.11.cloned.1.call-update
  311.7 0.2 reduce-scatter.3.cloned.1.call-start
  311.9 108.6 %all-gather.7.cloned.1.call-done = bf16[4096,1024]{1,0:T(8,128)(2,1)} async-done(((bf16[512,1024]{1,0:T(8,128)(2,1)}), bf16[4096,1024]{1,0:T(8,128)(2,1)}) %all-gather.7.cloned.1.call-update) | async-done | bytes 8388624 | tf_op jit(solution)/shard_map/all_gather | solution.py:106
  420.5 4.7 convolution_convert_fusion.5
  425.2 70.1 %all-gather.11.cloned.1.call-done = bf16[1024,2,1024]{0,2,1:T(8,128)(2,1)} async-done(((bf16[128,2,1024]{0,2,1:T(8,128)(2,1)}), bf16[1024,2,1024]{0,2,1:T(8,128)(2,1)}) %all-gather.11.cloned.1.call-update) | async-done | bytes 4194320 | tf_op jit(solution)/shard_map/all_gather | solution.py:124
  495.3 6.6 %conditional.1 = (f32[8,128]{1,0:T(8,128)S(1)}, f32[8,128,128]{1,2,0:T(8,128)S(1)}) conditional(s32[]{:T(128)} %convert_element_type.94, () %tuple.13, (s32[]{:T(128)}, s32[128]{0:T(128)S(1)}, bf16[128,1024]{1,0:T(8,128)(2,1)S(1)}, bf16[1024,2,1024]{0,2,1:T(8,128)(2,1)}) %tuple.14), branch_computations={%region_5.6_spmd, %region_6.9_spmd} | conditional | flops 550632576 | bytes 26502676 | solution.py:128
  495.3 0.1 iota_compare_fusion
  495.4 2.7 fusion.63
  498.1 1.1 fusion
  499.2 1.4 fusion.3
  500.6 1.3 fusion.2
  501.9 0.1 divide_convert_fusion
  502.0 5.8 %convolution_convert_fusion = bf16[128,4096]{1,0:T(8,128)(2,1)} fusion(bf16[128,1024]{0,1:T(8,128)(2,1)S(1)} %bitcast.63, bf16[1024,4096]{1,0:T(8,128)(2,1)} %param.22), kind=kOutput, calls=%fused_computation.21 | convolution fusion | flops 1074266112 | bytes 9699328 | tf_op jit(solution)/shard_map/dot_general | solution.py:137
  507.8 0.0 reduce-scatter.5.cloned.1.call-start
  507.8 23.1 %reduce-scatter.3.cloned.1.call-done = bf16[128,1024]{1,0:T(8,128)(2,1)} async-done(((bf16[128,4096]{1,0:T(8,128)(2,1)}), bf16[128,1024]{1,0:T(8,128)(2,1)}) %reduce-scatter.3.cloned.1.call-update) | async-done | bytes 262160 | tf_op jit(solution)/shard_map/reduce_scatter | solution.py:138
  530.9 1.0 add_convert_fusion
  532.0 3.4 collective-permute-start.1
  535.4 1.3 collective-permute-done.1
  536.7 2.7 convolution_convert_fusion.4
  539.4 21.0 %reduce-scatter.5.cloned.1.call-done = bf16[32,1024]{1,0:T(8,128)(2,1)} async-done(((bf16[128,1024]{1,0:T(8,128)(2,1)}), bf16[32,1024]{1,0:T(8,128)(2,1)}) %reduce-scatter.5.cloned.1.call-update) | async-done | bytes 65552 | tf_op jit(solution)/shard_map/reduce_scatter | solution.py:144
  560.4 0.8 convert_element_type.106
  561.3 0.9 fusion.38
  (32 shorter events, 0.1 us)
Async XLA Ops:
  6.5 22.4 %copy-start = (bf16[1024,1024]{1,0:T(8,128)(2,1)S(1)}, bf16[1024,1024]{1,0:T(8,128)(2,1)}, u32[]{:S(2)}) copy-start(bf16[1024,1024]{1,0:T(8,128)(2,1)} %param.17) | copy-start | bytes 6291460
  6.5 9.7 %copy-start.5 = (bf16[256,1024]{1,0:T(8,128)(2,1)S(1)}, bf16[256,1024]{1,0:T(8,128)(2,1)}, u32[]{:S(2)}) copy-start(bf16[256,1024]{1,0:T(8,128)(2,1)} %param.13) | copy-start | bytes 1572868
  6.5 9.7 %copy-start.9 = (f32[1024]{0:T(1024)S(1)}, f32[1024]{0:T(1024)}, u32[]{:S(2)}) copy-start(f32[1024]{0:T(1024)} %param.14) | copy-start | bytes 12292
  6.5 59.7 %all-gather.5.cloned.1.call-start = ((), (), s32[]{:S(2)}) async-start(), calls=%async_computation.2 | async-start | bytes 1310720 | tf_op jit(solution)/shard_map/all_gather | solution.py:101
  12.7 6.8 %collective-permute-start = (bf16[256,2048]{1,0:T(8,128)(2,1)}, bf16[256,2048]{1,0:T(8,128)(2,1)}, u32[]{:S(2)}, u32[]{:S(2)}) collective-permute-start(bf16[256,2048]{1,0:T(8,128)(2,1)} %convolution_convert_fusion.1), channel_id=1, source_target_pairs={{0,1},{1,2},{2,3},{3,4},{4,5},{5,6},{6,7},{7,8},{8,9},{9,10},{10,1... | collective-permute-start | bytes 3145736 | tf_op jit(solution)/shard_map/ppermute | solution.py:20
  25.6 2.5 copy-start.7
  28.1 1.0 copy-start.6
  28.1 18.9 %copy-start.4 = (bf16[1024,1024]{1,0:T(8,128)(2,1)S(1)}, bf16[1024,1024]{1,0:T(8,128)(2,1)}, u32[]{:S(2)}) copy-start(bf16[1024,1024]{1,0:T(8,128)(2,1)} %param.18) | copy-start | bytes 6291460
  48.1 247.6 %all-gather.9.cloned.1.call-start = ((), (), s32[]{:S(2)}) async-start(), calls=%async_computation.4 | async-start | bytes 18874368 | tf_op jit(solution)/shard_map/all_gather | solution.py:107
  48.9 371.6 %all-gather.7.cloned.1.call-start = ((), (), s32[]{:S(2)}) async-start(), calls=%async_computation.3 | async-start | bytes 9437184 | tf_op jit(solution)/shard_map/all_gather | solution.py:106
  49.6 445.7 %all-gather.11.cloned.1.call-start = ((), (), s32[]{:S(2)}) async-start(), calls=%async_computation.5 | async-start | bytes 4718592 | tf_op jit(solution)/shard_map/all_gather | solution.py:124
  295.7 12.3 %copy-start.2 = (bf16[128,4096]{1,0:T(8,128)(2,1)S(1)}, bf16[128,4096]{1,0:T(8,128)(2,1)}, u32[]{:S(2)}) copy-start(bf16[128,4096]{1,0:T(8,128)(2,1)} %all-gather.5.cloned.1.call-done) | copy-start | bytes 3145732
  295.7 12.3 %copy-start.8 = (f32[4096]{0:T(1024)S(1)}, f32[4096]{0:T(1024)}, u32[]{:S(2)}) copy-start(f32[4096]{0:T(1024)} %param.19) | copy-start | bytes 49156
  311.7 219.3 %reduce-scatter.3.cloned.1.call-start = ((), (), s32[]{:S(2)}) async-start(), calls=%async_computation.6 | async-start | bytes 1310720 | tf_op jit(solution)/shard_map/reduce_scatter | solution.py:138
  501.9 29.0 %copy-start.3 = (bf16[128,1024]{1,0:T(8,128)(2,1)S(1)}, bf16[128,1024]{1,0:T(8,128)(2,1)}, u32[]{:S(2)}) copy-start(bf16[128,1024]{1,0:T(8,128)(2,1)} %convolution_convert_fusion.6) | copy-start | bytes 786436
  502.0 60.3 %copy-start.1 = (bf16[1024,1024]{1,0:T(8,128)(2,1)S(1)}, bf16[1024,1024]{1,0:T(8,128)(2,1)}, u32[]{:S(2)}) copy-start(bf16[1024,1024]{1,0:T(8,128)(2,1)} %param.17) | copy-start | bytes 6291460
  507.8 52.6 %reduce-scatter.5.cloned.1.call-start = ((), (), s32[]{:S(2)}) async-start(), calls=%async_computation.7 | async-start | bytes 327680 | tf_op jit(solution)/shard_map/reduce_scatter | solution.py:144
  532.0 4.7 collective-permute-start.1
Sparse Core Ops, SparseCore 0:
  48.3 17.9 all-gather.4
  68.4 227.2 all-gather.8
  297.8 122.6 all-gather.6
  422.4 72.8 all-gather.10
  507.9 22.9 reduce-scatter.2
  539.5 20.8 reduce-scatter.4
where the time goes:
time: 570 us; the launch traced here: 569 us
  waiting for transfers between devices  470 us (82%)
  matrix products  31.1 us (5%)
  local copies, waits for them, and re-layouts  17.5 us (3%)
  blocking collectives  16.9 us (3%)
  between operations  13.7 us (2%)
  other arithmetic  12.6 us (2%)
  starting transfers between devices  7.15 us (1%)
    all_gather x1, waiting for transfers between devices, body(): keyval_rows = lax.all_gather(coarse_keyval, 'seq', axis=0, tiled=True)  228 us
    all_gather x1, waiting for transfers between devices, body(): query_rows = lax.all_gather(coarse_query, 'seq', axis=0, tiled=True)  109 us
    all_gather x1, waiting for transfers between devices, body(): piece = lax.all_gather(coarse_kv, 'seq', axis=0, tiled=True)  70.1 us
    reduce_scatter x1, waiting for transfers between devices, body(): lax.psum_scatter(partials.astype(jnp.bfloat16), 'tp', scatter_dimension=1...  23.1 us
    reduce_scatter x1, waiting for transfers between devices, body(): lax.psum_scatter(jnp.dot(delayed, up_weight, preferred_element_type=jnp.f...  21 us
    all_gather x1, blocking collectives, body(): pooled_all = lax.all_gather(pooled, 'tp', axis=0, tiled=True)  16.9 us
    all_gather x1, waiting for transfers between devices, body(): shortened = lax.all_gather(short_cols, 'tp', axis=1, tiled=True)  16.6 us
    unnamed x21, local copies, waits for them, and re-layouts  12.5 us
  transfers between devices with their start and end apart: 8, of which 7 were waited for; matrix products, arithmetic and copies ran while one was open for 4% of the time, Pallas kernels for 0%

commit v1 on v0

--- a/solution.py
+++ b/solution.py
@@ -151,9 +151,142 @@
     return result.astype(jnp.bfloat16)
 
 
+def head_attention(queries, keys, values):
+    count, columns = queries.shape
+    heads = columns // HEAD
+    scale = 1.0 / math.sqrt(HEAD)
+    outs = []
+    index = jnp.arange(count, dtype=jnp.int32)
+    allowed = index[None, :] <= index[:, None]
+    for head in range(heads):
+        part = slice(head * HEAD, (head + 1) * HEAD)
+        scores = (
+            jnp.dot(queries[:, part], keys[:, part].T, preferred_element_type=jnp.float32) * scale
+        )
+        scores = jnp.where(allowed, scores, big_negative)
+        peak = jnp.max(scores, axis=-1, keepdims=True)
+        terms = jnp.where(allowed, jnp.exp(scores - peak), 0.0)
+        denom = jnp.sum(terms, axis=-1, keepdims=True)
+        mixed = jnp.dot(
+            terms.astype(jnp.bfloat16), values[:, part], preferred_element_type=jnp.float32
+        )
+        outs.append((mixed / denom).astype(jnp.bfloat16))
+    return jnp.concatenate(outs, 1)
+
+
+def head_body(
+    tokens,
+    fine_gain,
+    fine_query,
+    fine_keyval,
+    fine_out,
+    down_weight,
+    coarse_gain,
+    coarse_query,
+    coarse_keyval,
+    coarse_out,
+    up_weight,
+):
+    seq = lax.axis_size("seq")
+    tok_rows, width = tokens.shape
+    fine_heads = width // HEAD
+    scale = 1.0 / math.sqrt(HEAD)
+    start_row = lax.axis_index(("seq", "tp")) * tok_rows
+    earlier = from_behind(tokens, ("seq", "tp"), 1)
+    down_all = lax.all_gather(down_weight, "tp", axis=1, tiled=True)
+    depth, local_cols = coarse_query.shape
+    own = local_cols // seq
+    stacked = jnp.concatenate(
+        [
+            coarse_query.reshape(depth, 1, seq, own),
+            coarse_keyval.reshape(depth, 2, seq, own),
+        ],
+        1,
+    )
+    stacked = jnp.transpose(stacked, (2, 0, 1, 3)).reshape(seq, depth, 3 * own)
+    weights = lax.all_to_all(stacked, "seq", 0, 0, tiled=True).reshape(seq * depth, 3 * own)
+    both = jnp.concatenate([earlier, tokens], 0).astype(jnp.float32)
+    normed = normalize(both, fine_gain).astype(jnp.bfloat16)
+    inputs = tokens.astype(jnp.float32)
+    queries = jnp.dot(
+        normed[tok_rows:], fine_query, preferred_element_type=jnp.float32
+    ).astype(jnp.bfloat16)
+    key_rows = jnp.dot(normed, fine_keyval, preferred_element_type=jnp.float32).astype(jnp.bfloat16)
+    span = key_rows.shape[0]
+    key_heads = key_rows[:, :width].reshape(span, fine_heads, HEAD)
+    value_heads = key_rows[:, width:].reshape(span, fine_heads, HEAD)
+    query_heads = queries.reshape(tok_rows, fine_heads, HEAD)
+    scores = (
+        jnp.einsum("qhd,khd->hqk", query_heads, key_heads, preferred_element_type=jnp.float32)
+        * scale
+    )
+    row_index = jnp.arange(tok_rows, dtype=jnp.int32)[:, None]
+    col_index = jnp.arange(span, dtype=jnp.int32)[None, :]
+    offset = row_index + WINDOW - col_index
+    allowed = (offset >= 0) & (offset < WINDOW) & (start_row - WINDOW + col_index >= 0)
+    scores = jnp.where(allowed[None], scores, big_negative)
+    peak = jnp.max(scores, axis=-1, keepdims=True)
+    terms = jnp.where(allowed[None], jnp.exp(scores - peak), 0.0)
+    denom = jnp.sum(terms, axis=-1)
+    mixed = jnp.einsum(
+        "hqk,khd->qhd", terms.astype(jnp.bfloat16), value_heads, preferred_element_type=jnp.float32
+    )
+    local = (mixed / jnp.transpose(denom)[..., None]).reshape(tok_rows, width).astype(jnp.bfloat16)
+    fine_state = (inputs + jnp.dot(local, fine_out, preferred_element_type=jnp.float32)).astype(
+        jnp.bfloat16
+    )
+    pooled = jnp.mean(
+        fine_state.astype(jnp.float32).reshape(tok_rows // SHORT, SHORT, width), axis=1
+    ).astype(jnp.bfloat16)
+    pooled_all = lax.all_gather(pooled, ("seq", "tp"), axis=0, tiled=True)
+    shortened = jnp.dot(pooled_all, down_all, preferred_element_type=jnp.float32).astype(
+        jnp.bfloat16
+    )
+    coarse_normed = normalize(shortened.astype(jnp.float32), coarse_gain).astype(jnp.bfloat16)
+    projected = jnp.dot(coarse_normed, weights, preferred_element_type=jnp.float32).astype(
+        jnp.bfloat16
+    )
+    heads_out = head_attention(
+        projected[:, :own], projected[:, own : 2 * own], projected[:, 2 * own :]
+    )
+    count = heads_out.shape[0]
+    coarse_rows = count // seq
+    coarse_heads = lax.all_to_all(
+        heads_out.reshape(seq, coarse_rows, own), "seq", 0, 0, tiled=True
+    )
+    coarse_heads = jnp.transpose(coarse_heads, (1, 0, 2)).reshape(coarse_rows, local_cols)
+    short_cols = lax.dynamic_slice(
+        shortened,
+        (lax.axis_index("seq") * coarse_rows, lax.axis_index("tp") * local_cols),
+        (coarse_rows, local_cols),
+    )
+    partials = jnp.dot(coarse_heads, coarse_out, preferred_element_type=jnp.float32)
+    attended = lax.psum_scatter(
+        partials.astype(jnp.bfloat16), "tp", scatter_dimension=1, tiled=True
+    ).astype(jnp.float32)
+    coarse_state = (short_cols.astype(jnp.float32) + attended).astype(jnp.bfloat16)
+    prior_row = from_behind(coarse_state[coarse_rows - 1 :], "seq", 1)
+    delayed = jnp.concatenate([prior_row, coarse_state[: coarse_rows - 1]], 0)
+    lifted = lax.psum_scatter(
+        jnp.dot(delayed, up_weight, preferred_element_type=jnp.float32).astype(jnp.bfloat16),
+        "tp",
+        scatter_dimension=0,
+        tiled=True,
+    ).astype(jnp.float32)
+    result = fine_state.astype(jnp.float32) + jnp.repeat(lifted, SHORT, axis=0)
+    return result.astype(jnp.bfloat16)
+
+
+def chosen(*args):
+    local_heads = args[7].shape[1] // HEAD
+    if local_heads % lax.axis_size("seq") == 0 and args[0].shape[0] == WINDOW:
+        return head_body(*args)
+    return body(*args)
+
+
 def solution(mesh):
     return jax.shard_map(
-        body,
+        chosen,
         mesh=mesh,
         in_specs=(
             P(("seq", "tp"), None),

time: 570 us -> 265 us (0.46)
  waiting for transfers between devices: 470 us -> 74.3 us
  blocking collectives: 16.9 us -> 108 us
  matrix products: 31.1 us -> 38.5 us
    all_gather x4 -> x2, waiting for transfers between devices: 423 us -> 26.9 us  [the longest x1 26.9 us: head_body(): down_all = lax.all_gather(down_weight, 'tp', axis=1, tiled=True)]
    all_to_all x0 -> x2, blocking collectives: none -> 108 us  [the longest x1 93.4 us: head_body(): lax.all_to_all(stacked, 'seq', 0, 0, tiled=True)]
    all_gather x1 -> x0, blocking collectives: 16.9 us -> none  [body(): pooled_all = lax.all_gather(pooled, 'tp', axis=0, tiled=True)]
    dot_general x11, matrix products: 29.8 us -> 38.5 us  [the longest x1 13.1 us: head_body(): jnp.dot(pooled_all, down_all, preferred_element_type=jnp.float32)]
  transfers between devices with their start and end apart: 8 -> 6, of which waited for: 7 -> 5; matrix products, arithmetic and copies ran while one was open for 4% -> 4% of each run, Pallas kernels for 0% -> 0%
where the time goes in v1:
time: 265 us; the launch traced here: 264 us
  blocking collectives  108 us (41%)
  waiting for transfers between devices  74.3 us (28%)
  matrix products  38.5 us (15%)
  local copies, waits for them, and re-layouts  14.1 us (5%)
  between operations  13.4 us (5%)
  other arithmetic  9.67 us (4%)
  starting transfers between devices  6.06 us (2%)
    all_to_all x1, blocking collectives, head_body(): lax.all_to_all(stacked, 'seq', 0, 0, tiled=True)  93.4 us
    all_gather x1, waiting for transfers between devices, head_body(): down_all = lax.all_gather(down_weight, 'tp', axis=1, tiled=True)  26.9 us
    reduce_scatter x1, waiting for transfers between devices, head_body(): lax.psum_scatter(partials.astype(jnp.bfloat16), 'tp', scatter_dimension=1...  23 us
    reduce_scatter x1, waiting for transfers between devices, head_body(): lax.psum_scatter(jnp.dot(delayed, up_weight, preferred_element_type=jnp.f...  21 us
    all_to_all x1, blocking collectives, head_body(): lax.all_to_all(heads_out.reshape(seq, coarse_rows, own), 'seq', 0, 0, til...  14.6 us
    dot_general x1, matrix products, head_body(): jnp.dot(pooled_all, down_all, preferred_element_type=jnp.float32)  13.1 us
    unnamed x21, local copies, waits for them, and re-layouts  7.63 us
    ppermute x2, starting transfers between devices, from_behind(): return lax.ppermute(array, axis, pairs)  5.93 us
  transfers between devices with their start and end apart: 6, of which 5 were waited for; matrix products, arithmetic and copies ran while one was open for 4% of the time, Pallas kernels for 0%

profile of v1, /device:TPU:0, one launch (start us, length us, event | category | flops | bytes accessed | tf_op | source)
XLA Modules:
  0.0 264.1 jit_solution(3443862918285150967)
XLA Ops:
  6.5 0.0 copy-start
  6.5 2.6 collective-permute-start
  9.1 0.2 fusion.53
  9.3 1.5 collective-permute-done
  10.8 1.3 fusion.12
  12.1 1.4 fusion.14
  13.5 0.0 copy-start.7
  13.5 4.7 %convolution_convert_fusion.2 = bf16[512,2048]{1,0:T(8,128)(2,1)S(1)} fusion(bf16[512,1024]{1,0:T(8,128)(2,1)S(1)} %fusion.14, bf16[1024,2048]{1,0:T(8,128)(2,1)} %param.14), kind=kOutput, calls=%fused_computation.19 | convolution fusion | flops 2148532224 | bytes 7340032 | tf_op jit(solution)/shard_map/dot_general | solution.py:214
  18.2 1.2 slice_bitcast_fusion
  19.4 0.0 copy-done.7
  19.4 1.5 fusion.35
  20.9 1.3 copy.29
  22.2 2.1 fusion.38
  24.4 2.5 fusion.67
  26.9 0.8 fusion.32
  27.7 0.2 copy-done.2
  27.9 1.7 fusion.36
  29.6 0.6 multiply_convert_fusion
  30.3 0.0 all-gather.3.cloned.1.call-update
  30.3 0.0 all-gather.5.cloned.1.call-start
  30.3 0.7 all-gather.5.cloned.1.call-update
  31.0 0.0 reduce-scatter.3.cloned.1.call-start
  31.1 4.7 %copy.25 = bf16[512,2,1024]{0,2,1:T(8,128)(2,1)S(1)} copy(bf16[512,2,1024]{2,1,0:T(2,128)(2,1)} %param.19) | data formatting | bytes 4194304 | tf_op args[8]
  35.8 1.5 copy.24
  37.3 0.3 maximum_bitcast_fusion
  37.6 0.2 copy.26
  37.8 93.4 %all_to_all.10 = bf16[8,512,384]{1,2,0:T(8,128)(2,1)} all-to-all(bf16[8,512,384]{1,2,0:T(8,128)(2,1)S(1)} %bitcast.49), channel_id=1, replica_groups=mesh['seq'=8,'tp'=4] {'seq'}, dimensions={0} | all-to-all | bytes 6291456 | tf_op jit(solution)/shard_map/all_to_all | solution.py:207
  131.2 4.7 %copy.27 = bf16[8,512,384]{2,1,0:T(8,128)(2,1)} copy(bf16[8,512,384]{1,2,0:T(8,128)(2,1)} %all_to_all.10) | data formatting | bytes 6291456 | tf_op jit(solution)/shard_map/all_to_all | solution.py:207
  136.0 26.9 %all-gather.5.cloned.1.call-done = bf16[1024,4096]{1,0:T(8,128)(2,1)} async-done(((bf16[1024,1024]{1,0:T(8,128)(2,1)}), bf16[1024,4096]{1,0:T(8,128)(2,1)}) %all-gather.5.cloned.1.call-update) | async-done | bytes 8388624 | tf_op jit(solution)/shard_map/all_gather | solution.py:196
  162.8 13.1 %fusion.1 = (f32[1024]{0:T(1024)S(1)}, bf16[1024,4096]{1,0:T(8,128)(2,1)S(1)}) fusion(bf16[1024,1024]{1,0:T(8,128)(2,1)} %all-gather.3.cloned.1.call-done, bf16[1024,4096]{1,0:T(8,128)(2,1)} %all-gather.5.cloned.1.call-done), kind=kOutput, calls=%fused_computation.3 | convolution fusion | flops 8606710784 | bytes 18878464 | tf_op jit(solution)/shard_map/dot_general | solution.py:242
  175.9 4.5 %fusion.22 = bf16[1024,384]{1,0:T(8,128)(2,1)S(1)} fusion(bf16[4096,384]{1,0:T(8,128)(2,1)S(1)} %bitcast.52, bf16[1024,4096]{1,0:T(8,128)(2,1)S(1)} %get-tuple-element.12, f32[4096]{0:T(1024)S(1)} %copy-done.8, f32[1024]{0:T(1024)S(1)} %add_rsqrt_fusion), kind=kOutput, calls=%fused_computation.33 | convolution fusion | flops 3238395904 | bytes 12341248 | tf_op jit(solution)/shard_map/dot_general | solution.py:246
  180.5 0.7 fusion.8
  181.2 0.5 fusion.10
  181.7 0.8 fusion.44
  182.5 0.2 copy.28
  182.7 14.6 %all_to_all.11 = bf16[8,128,128]{1,2,0:T(8,128)(2,1)S(1)} all-to-all(bf16[8,128,128]{1,2,0:T(8,128)(2,1)S(1)} %copy.28), channel_id=1, replica_groups=mesh['seq'=8,'tp'=4] {'seq'}, dimensions={0} | all-to-all | bytes 524288 | tf_op jit(solution)/shard_map/all_to_all | solution.py:254
  197.3 5.9 %convolution_convert_fusion.1 = bf16[128,4096]{1,0:T(8,128)(2,1)} fusion(bf16[128,1024]{0,1:T(8,128)(2,1)S(1)} %bitcast.53, bf16[1024,4096]{1,0:T(8,128)(2,1)} %param.20), kind=kOutput, calls=%fused_computation.10 | convolution fusion | flops 1074266112 | bytes 9699328 | tf_op jit(solution)/shard_map/dot_general | solution.py:263
  203.2 0.0 reduce-scatter.3.cloned.1.call-update
  203.2 0.0 reduce-scatter.5.cloned.1.call-start
  203.3 23.0 %reduce-scatter.3.cloned.1.call-done = bf16[128,1024]{1,0:T(8,128)(2,1)} async-done(((bf16[128,4096]{1,0:T(8,128)(2,1)}), bf16[128,1024]{1,0:T(8,128)(2,1)}) %reduce-scatter.3.cloned.1.call-update) | async-done | bytes 262160 | tf_op jit(solution)/shard_map/reduce_scatter | solution.py:264
  226.2 1.1 add_convert_fusion
  227.3 3.4 %collective-permute-start.1 = (bf16[1,1024]{1,0:T(2,128)(2,1)S(1)}, bf16[1,1024]{1,0:T(2,128)(2,1)S(1)}, u32[]{:S(2)}, u32[]{:S(2)}) collective-permute-start(bf16[1,1024]{1,0:T(2,128)(2,1)S(1)} %slice.38), channel_id=1, source_target_pairs={{0,4},{4,8},{8,12},{12,16},{16,20},{20,24},{24,28},{1,5},{5,9},{9,... | collective-permute-start | bytes 6152 | tf_op jit(solution)/shard_map/ppermute | solution.py:20
  230.7 1.3 collective-permute-done.1
  232.0 2.7 %convolution_convert_fusion.4 = bf16[128,1024]{1,0:T(8,128)(2,1)} fusion(bf16[1024,1024]{1,0:T(8,128)(2,1)} %param.21, bf16[127,1024]{1,0:T(8,128)(2,1)S(1)} %bitcast.54, bf16[1,1024]{1,0:T(2,128)(2,1)S(1)} %collective-permute-done.1), kind=kOutput, calls=%fused_computation.43 | convolution fusion | flops 269090816 | bytes 2621440 | tf_op jit(solution)/shard_map/dot_general | solution.py:271
  234.8 0.0 reduce-scatter.5.cloned.1.call-update
  234.8 21.0 %reduce-scatter.5.cloned.1.call-done = bf16[32,1024]{1,0:T(8,128)(2,1)} async-done(((bf16[128,1024]{1,0:T(8,128)(2,1)}), bf16[32,1024]{1,0:T(8,128)(2,1)}) %reduce-scatter.5.cloned.1.call-update) | async-done | bytes 65552 | tf_op jit(solution)/shard_map/reduce_scatter | solution.py:270
  255.8 0.8 convert_element_type.95
  256.6 0.9 fusion.37
  (21 shorter events, 0.1 us)
Async XLA Ops:
  6.5 21.2 %copy-start = (bf16[1024,1024]{1,0:T(8,128)(2,1)S(1)}, bf16[1024,1024]{1,0:T(8,128)(2,1)}, u32[]{:S(2)}) copy-start(bf16[1024,1024]{1,0:T(8,128)(2,1)} %param.15) | copy-start | bytes 6291460
  6.5 129.4 %all-gather.3.cloned.1.call-start = ((), (), s32[]{:S(2)}) async-start(), calls=%async_computation.4 | async-start | bytes 2162688 | tf_op jit(solution)/shard_map/all_gather | solution.py:241
  6.5 4.3 %collective-permute-start = (bf16[256,1024]{1,0:T(8,128)(2,1)}, bf16[256,1024]{1,0:T(8,128)(2,1)S(1)}, u32[]{:S(2)}, u32[]{:S(2)}) collective-permute-start(bf16[256,1024]{1,0:T(8,128)(2,1)} %param.11), channel_id=1, source_target_pairs={{0,1},{1,2},{2,3},{3,4},{4,5},{5,6},{6,7},{7,8},{8,9},{9,10},{10,1... | collective-permute-start | bytes 1572872 | tf_op jit(solution)/shard_map/ppermute | solution.py:20
  13.5 5.9 %copy-start.7 = (bf16[1024,1024]{1,0:T(8,128)(2,1)S(1)}, bf16[1024,1024]{1,0:T(8,128)(2,1)}, u32[]{:S(2)}) copy-start(bf16[1024,1024]{1,0:T(8,128)(2,1)} %param.13) | copy-start | bytes 6291460
  24.3 2.5 copy-start.5
  26.9 1.0 copy-start.2
  30.3 132.6 %all-gather.5.cloned.1.call-start = ((), (), s32[]{:S(2)}) async-start(), calls=%async_computation.5 | async-start | bytes 10485760 | tf_op jit(solution)/shard_map/all_gather | solution.py:196
  31.0 195.2 %reduce-scatter.3.cloned.1.call-start = ((), (), s32[]{:S(2)}) async-start(), calls=%async_computation.6 | async-start | bytes 1310720 | tf_op jit(solution)/shard_map/reduce_scatter | solution.py:264
  136.0 40.0 %copy-start.8 = (f32[4096]{0:T(1024)S(1)}, f32[4096]{0:T(1024)}, u32[]{:S(2)}) copy-start(f32[4096]{0:T(1024)} %param.17) | copy-start | bytes 49156
  162.8 13.1 %copy-start.3 = (bf16[8,512,384]{2,1,0:T(8,128)(2,1)S(1)}, bf16[8,512,384]{2,1,0:T(8,128)(2,1)}, u32[]{:S(2)}) copy-start(bf16[8,512,384]{2,1,0:T(8,128)(2,1)} %copy.27) | copy-start | bytes 9437188
  175.9 4.6 %copy-start.6 = (bf16[1024,4096]{1,0:T(8,128)(2,1)}, bf16[1024,4096]{1,0:T(8,128)(2,1)S(1)}, u32[]{:S(2)}) copy-start(bf16[1024,4096]{1,0:T(8,128)(2,1)S(1)} %get-tuple-element.12) | copy-start | bytes 25165828
  197.3 60.3 %copy-start.1 = (bf16[1024,1024]{1,0:T(8,128)(2,1)S(1)}, bf16[1024,1024]{1,0:T(8,128)(2,1)}, u32[]{:S(2)}) copy-start(bf16[1024,1024]{1,0:T(8,128)(2,1)} %param.15) | copy-start | bytes 6291460
  203.2 53.5 %copy-start.4 = (bf16[256,1024]{1,0:T(8,128)(2,1)S(1)}, bf16[256,1024]{1,0:T(8,128)(2,1)}, u32[]{:S(2)}) copy-start(bf16[256,1024]{1,0:T(8,128)(2,1)} %get-tuple-element.10) | copy-start | bytes 1572868
  203.2 52.6 %reduce-scatter.5.cloned.1.call-start = ((), (), s32[]{:S(2)}) async-start(), calls=%async_computation.7 | async-start | bytes 327680 | tf_op jit(solution)/shard_map/reduce_scatter | solution.py:270
  227.3 4.7 %collective-permute-start.1 = (bf16[1,1024]{1,0:T(2,128)(2,1)S(1)}, bf16[1,1024]{1,0:T(2,128)(2,1)S(1)}, u32[]{:S(2)}, u32[]{:S(2)}) collective-permute-start(bf16[1,1024]{1,0:T(2,128)(2,1)S(1)} %slice.38), channel_id=1, source_target_pairs={{0,4},{4,8},{8,12},{12,16},{16,20},{20,24},{24,28},{1,5},{5,9},{9,... | collective-permute-start | bytes 6152 | tf_op jit(solution)/shard_map/ppermute | solution.py:20
Sparse Core Ops, SparseCore 0:
  30.4 72.9 all-gather.2
  105.0 57.8 all-gather.4
  203.3 22.8 reduce-scatter.2
  234.9 20.8 reduce-scatter.4

commit v2 on v0

--- a/solution.py
+++ b/solution.py
@@ -1,8 +1,11 @@
+import functools
 import math
 
 import jax
 import jax.numpy as jnp
 from jax import lax
+from jax.experimental import pallas as pl
+from jax.experimental.pallas import tpu as pltpu
 from jax.sharding import PartitionSpec as P
 
 HEAD = 128
@@ -151,9 +154,436 @@
     return result.astype(jnp.bfloat16)
 
 
+def flip(index, bit):
+    return index + bit - 2 * bit * lax.rem(lax.div(index, jnp.int32(bit)), jnp.int32(2))
+
+
+def bits_of(size):
+    out, bit = [], size // 2
+    while bit:
+        out.append(bit)
+        bit //= 2
+    return out
+
+
+def dot32(left, right):
+    return jnp.dot(left, right, preferred_element_type=jnp.float32)
+
+
+def dot_t(left, right):
+    return lax.dot_general(
+        left, right, (((1,), (1,)), ((), ())), preferred_element_type=jnp.float32
+    )
+
+
+def section_kernel(
+    seq, tp,
+    tokens, fine_gain, fine_query, fine_keyval, fine_out, down_weight, coarse_gain, stacked,
+    coarse_out, up_weight,
+    result,
+    both, wq, wkv, wo, down_all, weights, wout, wup,
+    normed, queries, key_rows, local, fine_state, pooled_all, coarse_normed, projected,
+    heads_out, heads_in, coarse_heads, short_cols, send1, recv1, state, prior, send2, recv2,
+    load_sem, halo_s, halo_r, w_s, w_r, d_s, d_r, p_s, p_r, h_s, h_r, r1_s, r1_r, row_s, row_r,
+    r2_s, r2_r,
+):
+    me_s = lax.axis_index("seq")
+    me_t = lax.axis_index("tp")
+    rows, width = tokens.shape
+    scale = 1.0 / math.sqrt(HEAD)
+    total = seq * tp
+    lin = me_s * tp + me_t
+    after = lax.rem(lin + 1, total)
+    before = lax.rem(lin + total - 1, total)
+
+    def around(index, step, size):
+        return lax.rem(index + step, size)
+
+    def remote(src, dst, send, recv, device):
+        copy = pltpu.make_async_remote_copy(
+            src_ref=src, dst_ref=dst, send_sem=send, recv_sem=recv,
+            device_id=device, device_id_type=pl.DeviceIdType.MESH,
+        )
+        copy.start()
+        return copy
+
+    def load(src, dst, index):
+        copy = pltpu.make_async_copy(src, dst, load_sem.at[index])
+        copy.start()
+        return copy
+
+    def linear(index):
+        return {"seq": lax.div(index, tp), "tp": lax.rem(index, tp)}
+
+    barrier = pltpu.get_barrier_semaphore()
+    peers = [{"seq": around(me_s, d, seq)} for d in range(1, seq)]
+    peers += [{"tp": around(me_t, d, tp)} for d in range(1, tp)]
+    peers += [linear(after), linear(before)]
+    in_tokens = load(tokens, both.at[pl.ds(rows, rows)], 0)
+    in_wkv = load(fine_keyval, wkv, 1)
+    in_wq = load(fine_query, wq, 2)
+    in_wo = load(fine_out, wo, 3)
+    in_down = load(down_weight, down_all.at[me_t], 4)
+    in_w = load(stacked.at[me_s], weights.at[me_s], 5)
+    in_wout = load(coarse_out, wout, 6)
+    in_wup = load(up_weight, wup, 7)
+    for peer in peers:
+        pl.semaphore_signal(barrier, inc=1, device_id=peer, device_id_type=pl.DeviceIdType.MESH)
+    pl.semaphore_wait(barrier, len(peers))
+
+    halo = remote(tokens, both.at[pl.ds(0, rows)], halo_s, halo_r, linear(after))
+    order = sorted(range(1, seq), key=lambda d: abs(2 * d - seq))
+    w_copies = []
+
+    def send_weights(offsets):
+        for d in offsets:
+            dest = around(me_s, d, seq)
+            w_copies.append(
+                remote(
+                    stacked.at[dest], weights.at[me_s], w_s.at[d - 1], w_r.at[d - 1],
+                    {"seq": dest},
+                )
+            )
+
+    send_weights(order[: (seq + 1) // 2])
+    tp_bits = bits_of(tp)
+    d_first = [
+        remote(
+            down_weight, down_all.at[me_t], d_s.at[bit - 1], d_r.at[bit - 1],
+            {"tp": flip(me_t, bit)},
+        )
+        for bit in tp_bits
+    ]
+
+    gain = fine_gain[...]
+
+    def norm_rows(first):
+        values = both[pl.ds(first, rows), :].astype(jnp.float32)
+        normed[pl.ds(first, rows), :] = normalize(values, gain).astype(jnp.bfloat16)
+
+    in_tokens.wait()
+    norm_rows(rows)
+    in_wq.wait()
+    tile = 2 * HEAD
+
+    @pl.loop(0, width // tile)
+    def _(i):
+        cols = pl.ds(pl.multiple_of(i * tile, tile), tile)
+        queries[:, cols] = dot32(normed[rows:, :], wq[:, cols]).astype(jnp.bfloat16)
+
+    halo.wait()
+    norm_rows(0)
+    in_wkv.wait()
+
+    @pl.loop(0, 2 * width // tile)
+    def _(i):
+        cols = pl.ds(pl.multiple_of(i * tile, tile), tile)
+        key_rows[:, cols] = dot32(normed[...], wkv[:, cols]).astype(jnp.bfloat16)
+
+    row_index = lax.broadcasted_iota(jnp.int32, (rows, 2 * rows), 0)
+    col_index = lax.broadcasted_iota(jnp.int32, (rows, 2 * rows), 1)
+    offset = row_index + rows - col_index
+    allowed = (offset >= 0) & (offset < WINDOW) & (lin * rows - rows + col_index >= 0)
+
+    def attend(query, key, value, mask):
+        scores = jnp.where(mask, dot_t(query, key) * scale, big_negative)
+        peak = jnp.max(scores, axis=-1, keepdims=True)
+        terms = jnp.where(mask, jnp.exp(scores - peak), 0.0)
+        denom = jnp.sum(terms, axis=-1, keepdims=True)
+        return (dot32(terms.astype(jnp.bfloat16), value) / denom).astype(jnp.bfloat16)
+
+    @pl.loop(0, width // HEAD)
+    def _(h):
+        cols = pl.ds(pl.multiple_of(h * HEAD, HEAD), HEAD)
+        vcols = pl.ds(pl.multiple_of(width + h * HEAD, HEAD), HEAD)
+        local[:, cols] = attend(queries[:, cols], key_rows[:, cols], key_rows[:, vcols], allowed)
+
+    in_wo.wait()
+    pool_rows = rows // SHORT
+
+    @pl.loop(0, width // tile)
+    def _(i):
+        cols = pl.ds(pl.multiple_of(i * tile, tile), tile)
+        value = both[rows:, cols].astype(jnp.float32) + dot32(local[...], wo[:, cols])
+        value = value.astype(jnp.bfloat16)
+        fine_state[:, cols] = value
+        mean = jnp.mean(value.astype(jnp.float32).reshape(pool_rows, SHORT, tile), axis=1)
+        pooled_all[lin, :, cols] = mean.astype(jnp.bfloat16)
+
+    done = []
+    held = [lin]
+    count = 0
+    for axis, bits in (("seq", bits_of(seq)), ("tp", tp_bits)):
+        for bit in bits:
+            stride = bit * tp if axis == "seq" else bit
+            where = {axis: flip(me_s if axis == "seq" else me_t, bit)}
+            copies = []
+            for slot in held:
+                copies.append(
+                    remote(
+                        pooled_all.at[slot], pooled_all.at[slot], p_s.at[count], p_r.at[count],
+                        where,
+                    )
+                )
+                count += 1
+            if axis == "tp" and bit == tp_bits[0]:
+                send_weights(order[(seq + 1) // 2 :])
+            for copy in copies:
+                copy.wait_recv()
+            done += copies
+            held = held + [flip(slot, stride) for slot in held]
+    d_done = list(d_first)
+    for copy in d_first[:1]:
+        copy.wait_recv()
+    have = [tp_bits[0]]
+    index = tp - 1
+    extra = []
+    for k, bit in enumerate(tp_bits[1:]):
+        subs = list(have)
+        now = []
+        for sub in subs:
+            slot = me_t
+            for other in tp_bits:
+                if sub & other:
+                    slot = flip(slot, other)
+            number = bit + sub - 1
+            now.append(
+                remote(
+                    down_all.at[slot], down_all.at[slot], d_s.at[number], d_r.at[number],
+                    {"tp": flip(me_t, bit)},
+                )
+            )
+        d_first[k + 1].wait_recv()
+        for copy in now:
+            copy.wait_recv()
+        extra += now
+        have = have + [bit] + [bit + sub for sub in subs]
+    in_down.wait()
+
+    per = seq // 2 if seq > 1 else 1
+    crows = pool_rows * tp
+    block = 2 * crows
+    cgain = coarse_gain[...]
+
+    @pl.loop(0, seq // 2)
+    def _(i):
+        first = pl.multiple_of(i * block, block)
+        pooled = pooled_all[pl.ds(i * 2 * tp, 2 * tp)].reshape(block, width)
+        total_sq = jnp.zeros((block, 1), jnp.float32)
+        fcols = down_all.shape[2]
+        half = fcols // 2
+        for t in range(tp):
+            for u in range(2):
+                part = dot32(pooled, down_all[t, :, u * half : (u + 1) * half]).astype(jnp.bfloat16)
+                wide = part.astype(jnp.float32)
+                total_sq += jnp.sum(wide * wide, axis=-1, keepdims=True)
+                base = t * fcols + u * half
+                coarse_normed[pl.ds(first, block), base : base + half] = part
+        factor = lax.rsqrt(total_sq / (tp * fcols) + epsilon)
+        for t in range(2 * tp):
+            cols = slice(t * half, (t + 1) * half)
+            wide = coarse_normed[pl.ds(first, block), cols].astype(jnp.float32)
+            coarse_normed[pl.ds(first, block), cols] = (wide * factor * cgain[:, cols]).astype(
+                jnp.bfloat16
+            )
+
+    mine = pooled_all[pl.ds(me_s * tp, tp)].reshape(crows, width)
+    fcols = down_all.shape[2]
+    for u in range(2):
+        cols = slice(u * fcols // 2, (u + 1) * fcols // 2)
+        short_cols[:, cols] = dot32(mine, down_all[me_t, :, cols])
+    in_w.wait()
+    for copy in w_copies:
+        copy.wait_recv()
+    depth, three = weights.shape[1:]
+    own = three // 3
+
+    @pl.loop(0, seq // 2)
+    def _(i):
+        first = pl.multiple_of(i * block, block)
+        acc = jnp.zeros((block, three), jnp.float32)
+        for j in range(seq):
+            acc += dot32(
+                coarse_normed[pl.ds(first, block), j * depth : (j + 1) * depth], weights[j]
+            )
+        projected[pl.ds(first, block), :] = acc.astype(jnp.bfloat16)
+
+    for i in range(seq // 2):
+        extent = (i + 1) * block
+        r = lax.broadcasted_iota(jnp.int32, (block, extent), 0) + i * block
+        c = lax.broadcasted_iota(jnp.int32, (block, extent), 1)
+        for h in range(own // HEAD):
+            part = slice(h * HEAD, (h + 1) * HEAD)
+            kpart = slice(own + h * HEAD, own + (h + 1) * HEAD)
+            vpart = slice(2 * own + h * HEAD, 2 * own + (h + 1) * HEAD)
+            out = attend(
+                projected[i * block : extent, part], projected[:extent, kpart],
+                projected[:extent, vpart], c <= r,
+            )
+            heads_out[2 * i : 2 * i + 2, :, part] = out.reshape(2, crows, HEAD)
+
+    heads_in[me_s] = heads_out[me_s]
+    h_copies = []
+    for d in order:
+        dest = around(me_s, d, seq)
+        h_copies.append(
+            remote(
+                heads_out.at[dest], heads_in.at[me_s], h_s.at[d - 1], h_r.at[d - 1],
+                {"seq": dest},
+            )
+        )
+    in_wout.wait()
+    in_wup.wait()
+    for copy in h_copies:
+        copy.wait_recv()
+    for j in range(seq):
+        coarse_heads[:, j * own : (j + 1) * own] = heads_in[j]
+
+    def partial(t, store):
+        @pl.loop(0, fcols // tile)
+        def _(i):
+            cols = pl.ds(pl.multiple_of(i * tile, tile), tile)
+            wcols = pl.ds(pl.multiple_of(t * fcols + i * tile, tile), tile)
+            store(cols, dot32(coarse_heads[...], wout[:, wcols]))
+
+    tp_order = sorted(range(1, tp), key=lambda d: abs(2 * d - tp))
+    r1 = []
+    for d in tp_order:
+        dest = around(me_t, d, tp)
+
+        def put(cols, value, d=d):
+            send1[d - 1, :, cols] = value.astype(jnp.bfloat16)
+
+        partial(dest, put)
+        r1.append(
+            remote(
+                send1.at[d - 1], recv1.at[d - 1], r1_s.at[d - 1], r1_r.at[d - 1], {"tp": dest}
+            )
+        )
+
+    def keep(cols, value):
+        short_cols[:, cols] = short_cols[:, cols].astype(jnp.bfloat16).astype(jnp.float32) + value
+
+    partial(me_t, keep)
+    for copy in r1:
+        copy.wait_recv()
+    whole = short_cols[...]
+    for d in range(1, tp):
+        whole += recv1[d - 1].astype(jnp.float32)
+    state[...] = whole.astype(jnp.bfloat16)
+    slab = prior.shape[0]
+    row_copy = remote(
+        state.at[pl.ds(crows - slab, slab)], prior, row_s, row_r, {"seq": around(me_s, 1, seq)}
+    )
+    rolled = pltpu.roll(state[...].astype(jnp.float32), 1, 0)
+    row_copy.wait_recv()
+    previous = prior[...].astype(jnp.float32)[slab - 1 : slab, :]
+    previous = jnp.where(me_s > 0, previous, 0.0)
+    top = lax.broadcasted_iota(jnp.int32, rolled.shape, 0) == 0
+    delayed = jnp.where(top, previous, rolled).astype(jnp.bfloat16)
+    coarse_heads[...] = delayed
+
+    @pl.loop(0, width // tile)
+    def _(i):
+        cols = pl.ds(pl.multiple_of(i * tile, tile), tile)
+        short_cols[:, cols] = dot32(coarse_heads[...], wup[:, cols])
+
+    r2 = []
+    for d in tp_order:
+        dest = around(me_t, d, tp)
+        part = short_cols[pl.ds(pl.multiple_of(dest * pool_rows, pool_rows), pool_rows), :]
+        send2[d - 1] = part.astype(jnp.bfloat16)
+        r2.append(
+            remote(
+                send2.at[d - 1], recv2.at[d - 1], r2_s.at[d - 1], r2_r.at[d - 1], {"tp": dest}
+            )
+        )
+    lifted = short_cols[pl.ds(pl.multiple_of(me_t * pool_rows, pool_rows), pool_rows), :]
+    for copy in r2:
+        copy.wait_recv()
+    for d in range(1, tp):
+        lifted += recv2[d - 1].astype(jnp.float32)
+    spread = jnp.broadcast_to(lifted[:, None, :], (pool_rows, SHORT, width)).reshape(rows, width)
+    result[...] = (fine_state[...].astype(jnp.float32) + spread).astype(jnp.bfloat16)
+    for copy in w_copies + d_done + extra + done + h_copies + r1 + [row_copy] + r2:
+        copy.wait_send()
+
+
+def head_body(
+    tokens,
+    fine_gain,
+    fine_query,
+    fine_keyval,
+    fine_out,
+    down_weight,
+    coarse_gain,
+    coarse_query,
+    coarse_keyval,
+    coarse_out,
+    up_weight,
+):
+    seq, tp = lax.axis_size("seq"), lax.axis_size("tp")
+    rows, width = tokens.shape
+    depth, local_cols = coarse_query.shape
+    own = local_cols // seq
+    stacked = jnp.concatenate(
+        [
+            coarse_query.reshape(depth, 1, seq, own),
+            coarse_keyval.reshape(depth, 2, seq, own),
+        ],
+        1,
+    )
+    stacked = jnp.transpose(stacked, (2, 0, 1, 3)).reshape(seq, depth, 3 * own)
+    pool_rows = rows // SHORT
+    crows = pool_rows * tp
+    count = crows * seq
+    bf, f32 = jnp.bfloat16, jnp.float32
+    V = pltpu.VMEM
+    dma = lambda n: pltpu.SemaphoreType.DMA((n,))
+    one = pltpu.SemaphoreType.DMA
+    anywhere = pl.BlockSpec(memory_space=pl.ANY)
+    vmem = pl.BlockSpec(memory_space=pltpu.VMEM)
+    return pl.pallas_call(
+        functools.partial(section_kernel, seq, tp),
+        out_shape=jax.ShapeDtypeStruct((rows, width), bf),
+        in_specs=[anywhere, vmem, anywhere, anywhere, anywhere, anywhere, vmem, anywhere,
+                  anywhere, anywhere],
+        out_specs=vmem,
+        scratch_shapes=[
+            V((2 * rows, width), bf), V(fine_query.shape, bf), V(fine_keyval.shape, bf),
+            V(fine_out.shape, bf), V((tp,) + down_weight.shape, bf), V((seq, depth, 3 * own), bf),
+            V(coarse_out.shape, bf), V(up_weight.shape, bf),
+            V((2 * rows, width), bf), V((rows, width), bf), V((2 * rows, 2 * width), bf),
+            V((rows, width), bf), V((rows, width), bf), V((seq * tp, pool_rows, width), bf),
+            V((count, tp * local_cols), bf), V((count, 3 * own), bf),
+            V((seq, crows, own), bf), V((seq, crows, own), bf), V((crows, local_cols), bf),
+            V((crows, local_cols), f32), V((tp - 1, crows, local_cols), bf),
+            V((tp - 1, crows, local_cols), bf), V((crows, local_cols), bf), V((16, local_cols), bf),
+            V((tp - 1, pool_rows, width), bf), V((tp - 1, pool_rows, width), bf),
+            dma(8), one(()), one(()), dma(seq - 1), dma(seq - 1), dma(tp - 1), dma(tp - 1),
+            dma(seq * tp - 1), dma(seq * tp - 1), dma(seq - 1), dma(seq - 1),
+            dma(tp - 1), dma(tp - 1), one(()), one(()), dma(tp - 1), dma(tp - 1),
+        ],
+        compiler_params=pltpu.CompilerParams(
+            collective_id=0, has_side_effects=True, vmem_limit_bytes=62 * 1024 * 1024
+        ),
+    )(tokens, fine_gain[None], fine_query, fine_keyval, fine_out, down_weight, coarse_gain[None],
+      stacked, coarse_out, up_weight)
+
+
+def chosen(*args):
+    seq, tp = lax.axis_size("seq"), lax.axis_size("tp")
+    local_heads = args[7].shape[1] // HEAD
+    powers = seq & (seq - 1) == 0 and tp & (tp - 1) == 0 and seq > 1 and tp > 1
+    square = args[10].shape[0] == args[10].shape[1] == args[7].shape[1]
+    if local_heads % seq == 0 and args[0].shape[0] == WINDOW and powers and square:
+        return head_body(*args)
+    return body(*args)
+
+
 def solution(mesh):
     return jax.shard_map(
-        body,
+        chosen,
         mesh=mesh,
         in_specs=(
             P(("seq", "tp"), None),

time: 570 us -> 158 us (0.28)
  waiting for transfers between devices: 470 us -> 0 us
  Pallas kernels: 0 us -> 146 us
  matrix products: 31.1 us -> 0 us
  blocking collectives: 16.9 us -> 0 us
  between operations: 13.7 us -> 0.04 us
  other arithmetic: 12.6 us -> 0.27 us
  starting transfers between devices: 7.15 us -> 0 us
  local copies, waits for them, and re-layouts: 17.5 us -> 11.1 us
    all_gather x4 -> x0, waiting for transfers between devices: 423 us -> none  [the longest x1 228 us: body(): keyval_rows = lax.all_gather(coarse_keyval, 'seq', axis=0, tiled=True)]
    pallas_call x0 -> x1, Pallas kernels: none -> 146 us  [head_body(): pl.pallas_call(functools.partial(section_kernel, seq, tp), out_shape=jax....]
    reduce_scatter x2 -> x0, waiting for transfers between devices: 44.1 us -> none  [the longest x1 23.1 us: body(): lax.psum_scatter(partials.astype(jnp.bfloat16), 'tp', scatter_dimension=1...]
    dot_general x11 -> x0, matrix products: 29.8 us -> none  [the longest x1 5.81 us: body(): jnp.dot(coarse_heads, coarse_out, preferred_element_type=jnp.float32)]
    all_gather x1 -> x0, blocking collectives: 16.9 us -> none  [body(): pooled_all = lax.all_gather(pooled, 'tp', axis=0, tiled=True)]
    ppermute x2 -> x0, starting transfers between devices: 6.76 us -> none  [from_behind(): return lax.ppermute(array, axis, pairs)]
    unnamed x21 -> x3, local copies, waits for them, and re-layouts: 12.5 us -> 8.09 us
  transfers between devices with their start and end apart: 8 -> 0, of which waited for: 7 -> 0; matrix products, arithmetic and copies ran while one was open for 4% -> 0% of each run, Pallas kernels for 0% -> 0%
where the time goes in v2:
time: 158 us; the launch traced here: 157 us
  Pallas kernels  146 us (92%)
  local copies, waits for them, and re-layouts  11.1 us (7%)
    pallas_call x1, Pallas kernels, head_body(): pl.pallas_call(functools.partial(section_kernel, seq, tp), out_shape=jax....  146 us
    unnamed x3, local copies, waits for them, and re-layouts  8.09 us

profile of v2, /device:TPU:0, one launch (start us, length us, event | category | flops | bytes accessed | tf_op | source)
XLA Modules:
  0.0 157.3 jit_solution(8673801360179164861)
XLA Ops:
  0.0 1.5 copy.16
  1.5 4.7 %copy.17 = bf16[512,2,1024]{0,2,1:T(8,128)(2,1)S(1)} copy(bf16[512,2,1024]{2,1,0:T(2,128)(2,1)} %param.19) | data formatting | bytes 4194304 | tf_op args[8]
  6.2 0.3 maximum_bitcast_fusion
  6.5 0.2 copy.18
  6.7 2.8 %copy.19.stacked = bf16[8,512,384]{2,1,0:T(8,128)(2,1)} copy(bf16[8,512,384]{1,2,0:T(8,128)(2,1)S(1)} %bitcast.7) | data formatting | bytes 6291456 | tf_op jit(solution)/shard_map/reshape | solution.py:536
  9.5 145.9 %shard_map.109 = bf16[256,1024]{1,0:T(8,128)(2,1)} custom-call(bf16[256,1024]{1,0:T(8,128)(2,1)} %tokens.1, f32[1,1024]{1,0:T(1,128)} %bitcast.11, bf16[1024,1024]{1,0:T(8,128)(2,1)} %fine_query.1, bf16[1024,2048]{1,0:T(8,128)(2,1)} %fine_keyval.1, bf16[1024,1024]{1,0:T(8,128)(2,1)} %fine_out.1, bf16[1024,1024]{1,0:T(8,128)(2,1)} %down_weight.1, ...), custom_call_target="tpu_custom_call" | custom-call | tf_op jit(solution)/shard_map/pallas_call | solution.py:546
  155.4 1.9 %copy.21 = bf16[256,1024]{1,0:T(8,128)(2,1)} copy(bf16[256,1024]{1,0:T(8,128)(2,1)} %shard_map.109) | data formatting | bytes 1048576

commit v3 on v2

--- a/solution.py
+++ b/solution.py
@@ -178,11 +178,11 @@
 
 def section_kernel(
     seq, tp,
-    tokens, fine_gain, fine_query, fine_keyval, fine_out, down_weight, coarse_gain, stacked,
-    coarse_out, up_weight,
+    tokens, fine_gain, fine_query, fine_keyval, fine_out, down_weight, coarse_gain, coarse_query,
+    coarse_kv, coarse_out, up_weight,
     result,
     both, wq, wkv, wo, down_all, weights, wout, wup,
-    normed, queries, key_rows, local, fine_state, pooled_all, coarse_normed, projected,
+    normed, queries, key_rows, local, fine_state, pooled_all, coarse_normed, projected, sums,
     heads_out, heads_in, coarse_heads, short_cols, send1, recv1, state, prior, send2, recv2,
     load_sem, halo_s, halo_r, w_s, w_r, d_s, d_r, p_s, p_r, h_s, h_r, r1_s, r1_r, row_s, row_r,
     r2_s, r2_r,
@@ -224,7 +224,14 @@
     in_wq = load(fine_query, wq, 2)
     in_wo = load(fine_out, wo, 3)
     in_down = load(down_weight, down_all.at[me_t], 4)
-    in_w = load(stacked.at[me_s], weights.at[me_s], 5)
+    own = coarse_query.shape[1] // seq
+
+    def head_parts(dest):
+        cols = pl.ds(pl.multiple_of(dest * own, own), own)
+        sources = [coarse_query.at[:, cols], coarse_kv.at[0, :, cols], coarse_kv.at[1, :, cols]]
+        return [(part, weights.at[me_s, :, pl.ds(k * own, own)]) for k, part in enumerate(sources)]
+
+    in_w = [load(src, dst, 8 + k) for k, (src, dst) in enumerate(head_parts(me_s))]
     in_wout = load(coarse_out, wout, 6)
     in_wup = load(up_weight, wup, 7)
     for peer in peers:
@@ -233,20 +240,48 @@
 
     halo = remote(tokens, both.at[pl.ds(0, rows)], halo_s, halo_r, linear(after))
     order = sorted(range(1, seq), key=lambda d: abs(2 * d - seq))
-    w_copies = []
+    w_copies = {}
 
     def send_weights(offsets):
         for d in offsets:
             dest = around(me_s, d, seq)
-            w_copies.append(
+            w_copies[d] = [
                 remote(
-                    stacked.at[dest], weights.at[me_s], w_s.at[d - 1], w_r.at[d - 1],
-                    {"seq": dest},
+                    src, dst, w_s.at[3 * (d - 1) + k], w_r.at[3 * (d - 1) + k], {"seq": dest}
                 )
-            )
-
-    send_weights(order[: (seq + 1) // 2])
+                for k, (src, dst) in enumerate(head_parts(dest))
+            ]
+
+    early = (seq + 1) // 4
+    send_weights(order[:early])
     tp_bits = bits_of(tp)
+    gain = fine_gain[...]
+
+    def norm_rows(first):
+        values = both[pl.ds(first, rows), :].astype(jnp.float32)
+        normed[pl.ds(first, rows), :] = normalize(values, gain).astype(jnp.bfloat16)
+
+    in_tokens.wait()
+    norm_rows(rows)
+    in_wq.wait()
+    tile = 2 * HEAD
+
+    @pl.loop(0, width // tile)
+    def _(i):
+        cols = pl.ds(pl.multiple_of(i * tile, tile), tile)
+        queries[:, cols] = dot32(normed[rows:, :], wq[:, cols]).astype(jnp.bfloat16)
+
+    in_wkv.wait()
+
+    def project_rows(first):
+        @pl.loop(0, 2 * width // tile)
+        def _(i):
+            cols = pl.ds(pl.multiple_of(i * tile, tile), tile)
+            key_rows[pl.ds(first, rows), cols] = dot32(
+                normed[pl.ds(first, rows), :], wkv[:, cols]
+            ).astype(jnp.bfloat16)
+
+    project_rows(rows)
     d_first = [
         remote(
             down_weight, down_all.at[me_t], d_s.at[bit - 1], d_r.at[bit - 1],
@@ -254,31 +289,9 @@
         )
         for bit in tp_bits
     ]
-
-    gain = fine_gain[...]
-
-    def norm_rows(first):
-        values = both[pl.ds(first, rows), :].astype(jnp.float32)
-        normed[pl.ds(first, rows), :] = normalize(values, gain).astype(jnp.bfloat16)
-
-    in_tokens.wait()
-    norm_rows(rows)
-    in_wq.wait()
-    tile = 2 * HEAD
-
-    @pl.loop(0, width // tile)
-    def _(i):
-        cols = pl.ds(pl.multiple_of(i * tile, tile), tile)
-        queries[:, cols] = dot32(normed[rows:, :], wq[:, cols]).astype(jnp.bfloat16)
-
     halo.wait()
     norm_rows(0)
-    in_wkv.wait()
-
-    @pl.loop(0, 2 * width // tile)
-    def _(i):
-        cols = pl.ds(pl.multiple_of(i * tile, tile), tile)
-        key_rows[:, cols] = dot32(normed[...], wkv[:, cols]).astype(jnp.bfloat16)
+    project_rows(0)
 
     row_index = lax.broadcasted_iota(jnp.int32, (rows, 2 * rows), 0)
     col_index = lax.broadcasted_iota(jnp.int32, (rows, 2 * rows), 1)
@@ -326,8 +339,8 @@
                     )
                 )
                 count += 1
-            if axis == "tp" and bit == tp_bits[0]:
-                send_weights(order[(seq + 1) // 2 :])
+            if axis == "seq" and bit == bits[-1]:
+                send_weights(order[early:])
             for copy in copies:
                 copy.wait_recv()
             done += copies
@@ -392,21 +405,24 @@
     for u in range(2):
         cols = slice(u * fcols // 2, (u + 1) * fcols // 2)
         short_cols[:, cols] = dot32(mine, down_all[me_t, :, cols])
-    in_w.wait()
-    for copy in w_copies:
-        copy.wait_recv()
     depth, three = weights.shape[1:]
-    own = three // 3
-
-    @pl.loop(0, seq // 2)
-    def _(i):
-        first = pl.multiple_of(i * block, block)
-        acc = jnp.zeros((block, three), jnp.float32)
-        for j in range(seq):
-            acc += dot32(
-                coarse_normed[pl.ds(first, block), j * depth : (j + 1) * depth], weights[j]
-            )
-        projected[pl.ds(first, block), :] = acc.astype(jnp.bfloat16)
+
+    for d in [0] + order:
+        for copy in w_copies[d] if d else in_w:
+            copy.wait_recv() if d else copy.wait()
+        source = around(me_s, seq - d, seq)
+
+        @pl.loop(0, seq // 2)
+        def _(i, d=d, source=source):
+            at = pl.ds(pl.multiple_of(i * block, block), block)
+            cols = pl.ds(pl.multiple_of(source * depth, depth), depth)
+            product = dot32(coarse_normed[at, cols], weights[source])
+            if d == order[-1]:
+                projected[at, :] = (sums[at, :] + product).astype(jnp.bfloat16)
+            elif d:
+                sums[at, :] += product
+            else:
+                sums[at, :] = product
 
     for i in range(seq // 2):
         extent = (i + 1) * block
@@ -505,7 +521,8 @@
         lifted += recv2[d - 1].astype(jnp.float32)
     spread = jnp.broadcast_to(lifted[:, None, :], (pool_rows, SHORT, width)).reshape(rows, width)
     result[...] = (fine_state[...].astype(jnp.float32) + spread).astype(jnp.bfloat16)
-    for copy in w_copies + d_done + extra + done + h_copies + r1 + [row_copy] + r2:
+    w_flat = [copy for group in w_copies.values() for copy in group]
+    for copy in w_flat + d_done + extra + done + h_copies + r1 + [row_copy] + r2:
         copy.wait_send()
 
 
@@ -526,14 +543,6 @@
     rows, width = tokens.shape
     depth, local_cols = coarse_query.shape
     own = local_cols // seq
-    stacked = jnp.concatenate(
-        [
-            coarse_query.reshape(depth, 1, seq, own),
-            coarse_keyval.reshape(depth, 2, seq, own),
-        ],
-        1,
-    )
-    stacked = jnp.transpose(stacked, (2, 0, 1, 3)).reshape(seq, depth, 3 * own)
     pool_rows = rows // SHORT
     crows = pool_rows * tp
     count = crows * seq
@@ -547,7 +556,7 @@
         functools.partial(section_kernel, seq, tp),
         out_shape=jax.ShapeDtypeStruct((rows, width), bf),
         in_specs=[anywhere, vmem, anywhere, anywhere, anywhere, anywhere, vmem, anywhere,
-                  anywhere, anywhere],
+                  anywhere, anywhere, anywhere],
         out_specs=vmem,
         scratch_shapes=[
             V((2 * rows, width), bf), V(fine_query.shape, bf), V(fine_keyval.shape, bf),
@@ -555,12 +564,12 @@
             V(coarse_out.shape, bf), V(up_weight.shape, bf),
             V((2 * rows, width), bf), V((rows, width), bf), V((2 * rows, 2 * width), bf),
             V((rows, width), bf), V((rows, width), bf), V((seq * tp, pool_rows, width), bf),
-            V((count, tp * local_cols), bf), V((count, 3 * own), bf),
+            V((count, tp * local_cols), bf), V((count, 3 * own), bf), V((count, 3 * own), f32),
             V((seq, crows, own), bf), V((seq, crows, own), bf), V((crows, local_cols), bf),
             V((crows, local_cols), f32), V((tp - 1, crows, local_cols), bf),
             V((tp - 1, crows, local_cols), bf), V((crows, local_cols), bf), V((16, local_cols), bf),
             V((tp - 1, pool_rows, width), bf), V((tp - 1, pool_rows, width), bf),
-            dma(8), one(()), one(()), dma(seq - 1), dma(seq - 1), dma(tp - 1), dma(tp - 1),
+            dma(11), one(()), one(()), dma(3 * (seq - 1)), dma(3 * (seq - 1)), dma(tp - 1), dma(tp - 1),
             dma(seq * tp - 1), dma(seq * tp - 1), dma(seq - 1), dma(seq - 1),
             dma(tp - 1), dma(tp - 1), one(()), one(()), dma(tp - 1), dma(tp - 1),
         ],
@@ -568,7 +577,7 @@
             collective_id=0, has_side_effects=True, vmem_limit_bytes=62 * 1024 * 1024
         ),
     )(tokens, fine_gain[None], fine_query, fine_keyval, fine_out, down_weight, coarse_gain[None],
-      stacked, coarse_out, up_weight)
+      coarse_query, jnp.transpose(coarse_keyval, (1, 0, 2)), coarse_out, up_weight)
 
 
 def chosen(*args):

time: 158 us -> 143 us (0.905)
  Pallas kernels: 146 us -> 137 us
  local copies, waits for them, and re-layouts: 11.1 us -> 5.43 us
    pallas_call x1, Pallas kernels: 146 us -> 137 us  [head_body(): pl.pallas_call(functools.partial(section_kernel, seq, tp), out_shape=jax....]
    reshape x1 -> x0, local copies, waits for them, and re-layouts: 2.81 us -> none  [head_body(): stacked = jnp.transpose(stacked, (2, 0, 1, 3)).reshape(seq, depth, 3 * own)]
    unnamed x3 -> x2, local copies, waits for them, and re-layouts: 8.09 us -> 5.43 us
where the time goes in v3:
time: 143 us
  Pallas kernels  137 us (96%)
  local copies, waits for them, and re-layouts  5.43 us (4%)
    pallas_call x1, Pallas kernels, head_body(): pl.pallas_call(functools.partial(section_kernel, seq, tp), out_shape=jax....  137 us
    unnamed x2, local copies, waits for them, and re-layouts  5.43 us

profile of v3, /device:TPU:0, one launch (start us, length us, event | category | flops | bytes accessed | tf_op | source)
XLA Modules:
  0.0 142.5 jit_solution(2690940696814726916)
XLA Ops:
  0.0 3.6 %copy.14 = bf16[512,2,1024]{2,0,1:T(8,128)(2,1)} copy(bf16[512,2,1024]{2,1,0:T(2,128)(2,1)} %param.19) | data formatting | bytes 4194304 | tf_op args[8]
  3.6 137.1 %shard_map.109 = bf16[256,1024]{1,0:T(8,128)(2,1)} custom-call(bf16[256,1024]{1,0:T(8,128)(2,1)} %tokens.1, f32[1,1024]{1,0:T(1,128)} %bitcast.7, bf16[1024,1024]{1,0:T(8,128)(2,1)} %fine_query.1, bf16[1024,2048]{1,0:T(8,128)(2,1)} %fine_keyval.1, bf16[1024,1024]{1,0:T(8,128)(2,1)} %fine_out.1, bf16[1024,1024]{1,0:T(8,128)(2,1)} %down_weight.1, ...), custom_call_target="tpu_custom_call" | custom-call | tf_op jit(solution)/shard_map/pallas_call | solution.py:555
  140.7 1.9 %copy.16 = bf16[256,1024]{1,0:T(8,128)(2,1)} copy(bf16[256,1024]{1,0:T(8,128)(2,1)} %shard_map.109) | data formatting | bytes 1048576

commit v4 on v3

--- a/solution.py
+++ b/solution.py
@@ -463,29 +463,37 @@
             store(cols, dot32(coarse_heads[...], wout[:, wcols]))
 
     tp_order = sorted(range(1, tp), key=lambda d: abs(2 * d - tp))
-    r1 = []
-    for d in tp_order:
-        dest = around(me_t, d, tp)
-
-        def put(cols, value, d=d):
-            send1[d - 1, :, cols] = value.astype(jnp.bfloat16)
-
-        partial(dest, put)
-        r1.append(
-            remote(
-                send1.at[d - 1], recv1.at[d - 1], r1_s.at[d - 1], r1_r.at[d - 1], {"tp": dest}
+    r1 = {}
+    low_bits = tp_bits[::-1]
+    for k, bit in enumerate(low_bits):
+        for sub in range(tp - bit, 0, -2 * bit):
+            dest = me_t
+            for other in tp_bits:
+                if sub & other:
+                    dest = flip(dest, other)
+            for low in low_bits[:k]:
+                r1[sub + low].wait_recv()
+
+            def put(cols, value, sub=sub, k=k):
+                for low in low_bits[:k]:
+                    value += recv1[sub + low - 1, :, cols].astype(jnp.float32)
+                send1[sub - 1, :, cols] = value.astype(jnp.bfloat16)
+
+            partial(dest, put)
+            r1[sub] = remote(
+                send1.at[sub - 1], recv1.at[sub - 1], r1_s.at[sub - 1], r1_r.at[sub - 1],
+                {"tp": flip(me_t, bit)},
             )
-        )
 
     def keep(cols, value):
         short_cols[:, cols] = short_cols[:, cols].astype(jnp.bfloat16).astype(jnp.float32) + value
 
     partial(me_t, keep)
-    for copy in r1:
-        copy.wait_recv()
+    for bit in low_bits:
+        r1[bit].wait_recv()
     whole = short_cols[...]
-    for d in range(1, tp):
-        whole += recv1[d - 1].astype(jnp.float32)
+    for bit in low_bits:
+        whole += recv1[bit - 1].astype(jnp.float32)
     state[...] = whole.astype(jnp.bfloat16)
     slab = prior.shape[0]
     row_copy = remote(
@@ -522,7 +530,7 @@
     spread = jnp.broadcast_to(lifted[:, None, :], (pool_rows, SHORT, width)).reshape(rows, width)
     result[...] = (fine_state[...].astype(jnp.float32) + spread).astype(jnp.bfloat16)
     w_flat = [copy for group in w_copies.values() for copy in group]
-    for copy in w_flat + d_done + extra + done + h_copies + r1 + [row_copy] + r2:
+    for copy in w_flat + d_done + extra + done + h_copies + list(r1.values()) + [row_copy] + r2:
         copy.wait_send()
 
 

time: 143 us -> 140 us (0.979)
  Pallas kernels: 137 us -> 135 us
    pallas_call x1, Pallas kernels: 137 us -> 135 us  [head_body(): pl.pallas_call(functools.partial(section_kernel, seq, tp), out_shape=jax....]
where the time goes in v4:
time: 140 us
  Pallas kernels  135 us (96%)
  local copies, waits for them, and re-layouts  5.43 us (4%)
    pallas_call x1, Pallas kernels, head_body(): pl.pallas_call(functools.partial(section_kernel, seq, tp), out_shape=jax....  135 us
    unnamed x2, local copies, waits for them, and re-layouts  5.43 us

profile of v4, /device:TPU:0, one launch (start us, length us, event | category | flops | bytes accessed | tf_op | source)
XLA Modules:
  0.0 140.0 jit_solution(17684038987049047123)
XLA Ops:
  0.0 3.6 %copy.14 = bf16[512,2,1024]{2,0,1:T(8,128)(2,1)} copy(bf16[512,2,1024]{2,1,0:T(2,128)(2,1)} %param.19) | data formatting | bytes 4194304 | tf_op args[8]
  3.6 134.6 %shard_map.109 = bf16[256,1024]{1,0:T(8,128)(2,1)} custom-call(bf16[256,1024]{1,0:T(8,128)(2,1)} %tokens.1, f32[1,1024]{1,0:T(1,128)} %bitcast.7, bf16[1024,1024]{1,0:T(8,128)(2,1)} %fine_query.1, bf16[1024,2048]{1,0:T(8,128)(2,1)} %fine_keyval.1, bf16[1024,1024]{1,0:T(8,128)(2,1)} %fine_out.1, bf16[1024,1024]{1,0:T(8,128)(2,1)} %down_weight.1, ...), custom_call_target="tpu_custom_call" | custom-call | tf_op jit(solution)/shard_map/pallas_call | solution.py:563
  138.2 1.9 %copy.16 = bf16[256,1024]{1,0:T(8,128)(2,1)} copy(bf16[256,1024]{1,0:T(8,128)(2,1)} %shard_map.109) | data formatting | bytes 1048576
